TPU v7x, 8 devices: a whole 2x2x1 slice. The times are simulated.
8 devices in a mesh: gp: 8 (over z, y, x, core).
Axes of the slice: x: 2, y: 2, z: 1, core: 2. Of those that a mesh axis runs over, the one named last changes fastest.
Arguments:
- grid_in: bfloat16 [12288, 272], P('gp')
- mesh_static: bfloat16 [1024, 3], P('gp')
- edge_static: bfloat16 [18432, 4], P('gp')
- send_rows: int32 [64, 192], P('gp')
- edge_src: int32 [18432], P('gp')
- edge_dst: int32 [18432], P('gp')
- w_grid_in: bfloat16 [272, 512], replicated
- w_mesh_in: bfloat16 [3, 512], replicated
- w_edge_in: bfloat16 [4, 512], replicated
- w_edge_up: bfloat16 [1536, 512], replicated
- w_mesh_up: bfloat16 [1024, 512], replicated
- w_grid_up: bfloat16 [512, 512], replicated
- w_second: bfloat16 [6, 512, 512], replicated
- vectors: float32 [6, 4, 512], replicated
- d_mesh_out: bfloat16 [1024, 512], P('gp')
- d_grid_out: bfloat16 [12288, 512], P('gp')
Outputs:
- output 1: bfloat16 [1024, 512], P('gp')
- output 2: bfloat16 [12288, 512], P('gp')
- output 3: float32 [12288, 272], P('gp')
- output 4: float32 [272, 512], replicated
- output 5: float32 [3, 512], replicated
- output 6: float32 [4, 512], replicated
- output 7: float32 [1536, 512], replicated
- output 8: float32 [1024, 512], replicated
- output 9: float32 [512, 512], replicated
- output 10: float32 [6, 512, 512], replicated
- output 11: float32 [6, 4, 512], replicated
All inputs are finite; a program needn't handle non-finite values.
Results may differ from a plain program's by a relative error of at most 0.0196952.
Values are sent between devices in bfloat16 or wider.
A program may use at most 1 GiB of HBM per device.

v0:
```python
import jax
import jax.numpy as jnp
from jax import lax
from jax.sharding import PartitionSpec as P

LN_EPS = 1e-5
AXIS_NAME = 'gp'


def matmul(lhs, rhs):
    return jnp.dot(lhs, rhs, preferred_element_type=jnp.float32)


def contract_rows(lhs, rhs):
    return lax.dot_general(lhs, rhs, (((0,), (0,)), ((), ())), preferred_element_type=jnp.float32)


def contract_cols(lhs, rhs):
    return lax.dot_general(lhs, rhs, (((1,), (1,)), ((), ())), preferred_element_type=jnp.float32)


def mlp_tail(pre_act, w_two, vec_rows):
    pre_bias = pre_act + vec_rows[0]
    hidden = jax.nn.silu(pre_bias).astype(jnp.bfloat16)
    out_lin = matmul(hidden, w_two) + vec_rows[1]
    centered = out_lin - jnp.mean(out_lin, axis=-1, keepdims=True)
    inv_std = lax.rsqrt(jnp.mean(centered * centered, axis=-1, keepdims=True) + LN_EPS)
    normed = centered * inv_std
    return normed * vec_rows[2] + vec_rows[3], (pre_bias, hidden, normed, inv_std)


def mlp_tail_back(saved, w_two, vec_rows, d_out):
    pre_bias, hidden, normed, inv_std = saved
    d_normed = d_out * vec_rows[2]
    d_lin = inv_std * (d_normed - jnp.mean(d_normed, axis=-1, keepdims=True) - normed * jnp.mean(d_normed * normed, axis=-1, keepdims=True))
    d_lin_bf = d_lin.astype(jnp.bfloat16)
    d_w_two = contract_rows(hidden, d_lin_bf)
    d_hidden = contract_cols(d_lin_bf, w_two)
    sig_pre = jax.nn.sigmoid(pre_bias)
    d_pre = d_hidden * sig_pre * (1.0 + pre_bias * (1.0 - sig_pre))
    d_vec = jnp.stack([jnp.sum(d_pre, axis=0), jnp.sum(d_lin, axis=0), jnp.sum(d_out * normed, axis=0), jnp.sum(d_out, axis=0)])
    return d_pre.astype(jnp.bfloat16), d_w_two, d_vec


def solution(mesh):
    row_spec = P(AXIS_NAME, None)
    edge_spec = P(AXIS_NAME)
    rep_spec = P()
    in_specs = (row_spec, row_spec, row_spec, row_spec, edge_spec, edge_spec) + (rep_spec,) * 8 + (row_spec, row_spec)
    out_specs = (row_spec, row_spec, row_spec) + (rep_spec,) * 8

    def local_step(grid_in, mesh_static, edge_static, send_rows, edge_src, edge_dst, w_grid_in, w_mesh_in, w_edge_in, w_edge_up, w_mesh_up, w_grid_up, w_second, vectors, d_mesh_out, d_grid_out):
        latent = w_grid_up.shape[0]
        grid_rows = grid_in.shape[0]
        mesh_rows = mesh_static.shape[0]
        slot_rows = send_rows.size
        send_flat = send_rows.reshape(-1)
        up_edge = w_edge_up[:latent]
        up_send = w_edge_up[latent:2 * latent]
        up_recv = w_edge_up[2 * latent:]
        node_self = w_mesh_up[:latent]
        node_agg = w_mesh_up[latent:]

        grid_emb, grid_save = mlp_tail(matmul(grid_in, w_grid_in), w_second[0], vectors[0])
        grid_lat = grid_emb.astype(jnp.bfloat16)
        mesh_emb, mesh_save = mlp_tail(matmul(mesh_static, w_mesh_in), w_second[1], vectors[1])
        mesh_lat = mesh_emb.astype(jnp.bfloat16)
        edge_emb, edge_save = mlp_tail(matmul(edge_static, w_edge_in), w_second[2], vectors[2])
        edge_lat = edge_emb.astype(jnp.bfloat16)

        outgoing = jnp.take(grid_lat, send_flat, axis=0)
        incoming = lax.all_to_all(outgoing, AXIS_NAME, 0, 0, tiled=True)

        edge_pre = (matmul(edge_lat, up_edge)
                    + jnp.take(matmul(incoming, up_send), edge_src, axis=0)
                    + jnp.take(matmul(mesh_lat, up_recv), edge_dst, axis=0))
        edge_upd, upd_save = mlp_tail(edge_pre, w_second[3], vectors[3])
        edge_new = (edge_lat.astype(jnp.float32) + edge_upd).astype(jnp.bfloat16)
        agg_sum = jax.ops.segment_sum(edge_new.astype(jnp.float32), edge_dst, num_segments=mesh_rows).astype(jnp.bfloat16)
        node_upd, node_save = mlp_tail(matmul(mesh_lat, node_self) + matmul(agg_sum, node_agg), w_second[4], vectors[4])
        mesh_out = (mesh_lat.astype(jnp.float32) + node_upd).astype(jnp.bfloat16)
        cell_upd, cell_save = mlp_tail(matmul(grid_lat, w_grid_up), w_second[5], vectors[5])
        grid_out = (grid_lat.astype(jnp.float32) + cell_upd).astype(jnp.bfloat16)

        d_grid_top = d_grid_out.astype(jnp.float32)
        d_mesh_top = d_mesh_out.astype(jnp.float32)
        d_pre5, d_two5, d_vec5 = mlp_tail_back(cell_save, w_second[5], vectors[5], d_grid_top)
        d_w_grid_up = contract_rows(grid_lat, d_pre5)
        d_grid_lat = d_grid_top + contract_cols(d_pre5, w_grid_up)
        d_pre4, d_two4, d_vec4 = mlp_tail_back(node_save, w_second[4], vectors[4], d_mesh_top)
        d_w_mesh_up = jnp.concatenate([contract_rows(mesh_lat, d_pre4), contract_rows(agg_sum, d_pre4)], axis=0)
        d_mesh_lat = d_mesh_top + contract_cols(d_pre4, node_self)
        d_agg = contract_cols(d_pre4, node_agg)
        d_edge_new = jnp.take(d_agg, edge_dst, axis=0)
        d_pre3, d_two3, d_vec3 = mlp_tail_back(upd_save, w_second[3], vectors[3], d_edge_new)
        d_pre3_wide = d_pre3.astype(jnp.float32)
        d_slot_pre = jax.ops.segment_sum(d_pre3_wide, edge_src, num_segments=slot_rows).astype(jnp.bfloat16)
        d_node_pre = jax.ops.segment_sum(d_pre3_wide, edge_dst, num_segments=mesh_rows).astype(jnp.bfloat16)
        d_w_edge_up = jnp.concatenate([contract_rows(edge_lat, d_pre3), contract_rows(incoming, d_slot_pre), contract_rows(mesh_lat, d_node_pre)], axis=0)
        d_edge_lat = d_edge_new + contract_cols(d_pre3, up_edge)
        d_mesh_lat = d_mesh_lat + contract_cols(d_node_pre, up_recv)
        d_incoming = contract_cols(d_slot_pre, up_send).astype(jnp.bfloat16)
        d_outgoing = lax.all_to_all(d_incoming, AXIS_NAME, 0, 0, tiled=True)
        d_grid_lat = d_grid_lat + jax.ops.segment_sum(d_outgoing.astype(jnp.float32), send_flat, num_segments=grid_rows)
        d_pre2, d_two2, d_vec2 = mlp_tail_back(edge_save, w_second[2], vectors[2], d_edge_lat)
        d_w_edge_in = contract_rows(edge_static, d_pre2)
        d_pre1, d_two1, d_vec1 = mlp_tail_back(mesh_save, w_second[1], vectors[1], d_mesh_lat)
        d_w_mesh_in = contract_rows(mesh_static, d_pre1)
        d_pre0, d_two0, d_vec0 = mlp_tail_back(grid_save, w_second[0], vectors[0], d_grid_lat)
        d_w_grid_in = contract_rows(grid_in, d_pre0)
        d_grid_in = contract_cols(d_pre0, w_grid_in)

        weight_grads = (d_w_grid_in, d_w_mesh_in, d_w_edge_in, d_w_edge_up, d_w_mesh_up, d_w_grid_up,
                        jnp.stack([d_two0, d_two1, d_two2, d_two3, d_two4, d_two5]),
                        jnp.stack([d_vec0, d_vec1, d_vec2, d_vec3, d_vec4, d_vec5]))
        weight_grads = lax.psum(weight_grads, AXIS_NAME)
        return (mesh_out, grid_out, d_grid_in) + weight_grads

    return jax.shard_map(local_step, mesh=mesh, in_specs=in_specs, out_specs=out_specs, check_vma=False)
```

profile of v0, /device:TPU:0, one launch (start us, length us, event | category | flops | bytes accessed | tf_op | source)
XLA Modules:
  0.0 475.0 jit_solution(4920181912993281947)
XLA Ops:
  8.8 1.6 fusion.123
  10.4 2.0 convolution_add_fusion.5
  12.4 2.6 fusion.127
  16.8 1.6 add_convert_fusion.3
  18.4 1.7 copy.34
  20.1 5.4 %gather_fusion = bf16[1536,512]{1,0:T(8,128)(2,1)} fusion(bf16[1536,512]{1,0:T(8,128)(2,1)S(1)} %copy.34, s32[2048]{0:T(1024)S(1)} %pad_clamp_fusion.2), kind=kCustom, calls=%fused_computation.2 | custom fusion | bytes 3151872 | tf_op jit(solution)/shard_map/jit(_take)/gather | solution.py:71
  25.6 2.9 broadcast_select_fusion
  28.5 4.7 all-to-all-start
  36.1 1.5 fusion.125
  40.2 1.7 copy.36
  42.0 3.0 convolution_add_fusion.7
  45.0 2.6 fusion.130
  49.4 4.2 fusion.134
  54.7 2.7 convert_add_fusion
  57.4 3.5 copy.39
  61.8 5.4 %fusion.126 = (f32[2304]{0:T(1024)S(1)}, f32[2304,512]{0,1:T(8,128)}) fusion(f32[512]{0:T(512)S(1)} %bitcast.277, bf16[6,512,512]{2,1,0:T(8,128)(2,1)} %param.30, f32[2304,512]{1,0:T(8,128)S(1)} %convolution_add_fusion.4), kind=kOutput, calls=%fused_computation.262 | convolution fusion | flops 1216214784 | bytes 9972736 | tf_op jit(solution)/shard_map/dot_general | solution.py:11
  67.2 7.5 %gather_fusion.2 = f32[2304,512]{1,0:T(8,128)} fusion(f32[128,512]{1,0:T(8,128)S(1)} %fusion.74, s32[3072]{0:T(1024)S(1)} %get-tuple-element.130), kind=kCustom, calls=%fused_computation.clone | custom fusion | bytes 9446400 | tf_op jit(solution)/shard_map/jit(_take)/gather | solution.py:76
  74.7 3.0 multiply_reduce_fusion.5
  78.0 1.9 fusion.47
  79.9 3.1 add_convert_fusion.1
  83.0 5.0 %fusion.77 = f32[1536,512]{1,0:T(8,128)} fusion(bf16[1536,512]{1,0:T(8,128)(2,1)} %bitcast.16, bf16[1536,512]{1,0:T(8,128)(2,1)} %param.27), kind=kOutput, calls=%fused_computation.153 | convolution fusion | flops 805306368 | bytes 5242880 | tf_op jit(solution)/shard_map/dot_general | solution.py:11
  88.0 9.9 %gather_fusion.1 = f32[2304,512]{1,0:T(8,128)} fusion(f32[1536,512]{1,0:T(8,128)} %fusion.77, s32[3072]{0:T(1024)S(1)} %get-tuple-element.131), kind=kCustom, calls=%fused_computation.3 | custom fusion | bytes 9446400 | tf_op jit(solution)/shard_map/jit(_take)/gather | solution.py:75
  97.9 5.6 %fusion.7 = f32[2304,512]{1,0:T(8,128)S(1)} fusion(bf16[2304,512]{0,1:T(8,128)(2,1)S(1)} %add_convert_fusion.1, f32[2304,512]{1,0:T(8,128)} %gather_fusion.2, f32[2304,512]{1,0:T(8,128)} %gather_fusion.1, f32[512]{0:T(512)} %bitcast.274, pred[2304]{0:T(1024)(128)(4,1)S(1)} %get-tuple-element.132, pred[2304]{0:T(1024)(128)(4,1)S(1)} %copy-done.78, ...), kind=kOutput, calls=%fused_computation.26 | convolution fusion | flops 1213857792 | bytes 17046016 | tf_op jit(solution)/shard_map/dot_general | solution.py:11
  103.5 3.4 fusion.128
  107.5 1.7 copy-done.3
  109.1 3.4 fusion.19
  112.6 6.2 %copy.35 = f32[2304,512]{1,0:T(8,128)} copy(f32[2304,512]{0,1:T(8,128)} %fusion.19) | data formatting | bytes 9437184 | tf_op jit(solution)/shard_map/convert_element_type | solution.py:79
  118.8 16.5 %scatter_custom_fusion = f32[128,512]{1,0:T(8,128)S(1)} fusion(s32[2304]{0:T(1024)S(1)} %copy-done.59, f32[2304,512]{1,0:T(8,128)} %copy.35, f32[]{:T(128)} %constant.80.clone.1), kind=kCustom, calls=%fused_computation.192 | custom fusion | flops 1179648 | bytes 262656 | tf_op jit(solution)/shard_map/scatter-add | solution.py:79
  138.1 1.5 fusion.115
  139.5 2.0 fusion.122
  145.5 7.0 %gather_fusion.3 = f32[2304,512]{1,0:T(8,128)} fusion(f32[128,512]{1,0:T(8,128)S(1)} %fusion.68, s32[3072]{0:T(1024)S(1)} %get-tuple-element.130), kind=kCustom, calls=%fused_computation.1.clone | custom fusion | bytes 9446400 | tf_op jit(solution)/shard_map/jit(_take)/gather | solution.py:94
  152.5 6.2 %copy.38 = f32[2304,512]{0,1:T(8,128)} copy(f32[2304,512]{1,0:T(8,128)} %gather_fusion.3) | data formatting | bytes 9437184 | tf_op jit(solution)/shard_map/jit(_take)/gather | solution.py:94
  158.7 6.7 %multiply_reduce_fusion = (f32[512]{0:T(512)S(1)}, f32[2304]{0:T(1024)S(1)}, f32[2304]{0:T(1024)S(1)}, f32[512]{0:T(512)}) fusion(f32[2304,512]{0,1:T(8,128)} %copy.38, f32[2304,512]{0,1:T(8,128)} %copy-done.3, f32[2304]{0:T(1024)S(1)} %add_rsqrt_fusion, f32[2304]{0:T(1024)S(1)} %broadcast_multiply_fusion.4, pred[2304]{0:T(1024)(128)(4,1)S(1)} %get-tuple-element.132, ...), kind=kLoop, calls=%fused_computation.27 | loop fusion | flops 11790848 | bytes 9482496 | tf_op jit(solution)/shard_map/reduce_sum | solution.py:41
  165.4 1.9 fusion.117
  167.4 4.6 fusion.121
  172.1 6.0 %multiply_reduce_fusion.1 = (f32[512]{0:T(512)}, f32[2304]{0:T(1024)S(1)}, f32[2304]{0:T(1024)}, f32[512]{0:T(512)}, f32[2304,512]{0,1:T(8,128)}) fusion(f32[2304,512]{0,1:T(8,128)S(1)} %bitcast.210, f32[2304]{0:T(1024)S(1)} %add_rsqrt_fusion.1, f32[2304]{0:T(1024)S(1)} %broadcast_multiply_fusion.5, f32[512]{0:T(512)S(1)} %bitcast.238, ...), kind=kOutput, calls=%fused_computation.28 | convolution fusion | flops 1220930048 | bytes 17084672 | tf_op jit(solution)/shard_map/dot_general | solution.py:19
  178.1 17.1 %scatter_custom_fusion.3 = f32[128,512]{1,0:T(8,128)} fusion(s32[2304]{0:T(1024)S(1)} %copy-done.59, bf16[2304,512]{1,0:T(8,128)(2,1)S(1)} %get-tuple-element.77, f32[]{:T(128)} %constant.80.clone.1), kind=kCustom, calls=%fused_computation.8 | custom fusion | flops 2359296 | bytes 2621444 | tf_op jit(solution)/shard_map/scatter-add | solution.py:98
  195.2 18.0 %scatter_custom_fusion.1 = f32[1536,512]{1,0:T(8,128)} fusion(s32[2304]{0:T(1024)S(1)} %copy-done.60, bf16[2304,512]{1,0:T(8,128)(2,1)S(1)} %get-tuple-element.77, f32[]{:T(128)} %constant.80.clone.1), kind=kCustom, calls=%fused_computation.10 | custom fusion | flops 2359296 | bytes 5505028 | tf_op jit(solution)/shard_map/scatter-add | solution.py:97
  213.2 4.5 fusion.44
  217.8 2.2 convolution_convert_fusion
  222.3 3.1 all-to-all-start.1
  225.5 1.9 fusion.119
  227.4 3.2 pad_maximum_fusion.1
  232.4 3.2 pad_maximum_fusion
  235.6 1.6 fusion.118
  237.3 9.1 %all-to-all-done.1 = bf16[8,192,512]{2,1,0:T(8,128)(2,1)} async-done(((bf16[8,192,512]{2,1,0:T(8,128)(2,1)}), bf16[8,192,512]{2,1,0:T(8,128)(2,1)}, u32[]{:S(2)}, u32[]{:S(2)}) %all-to-all-start.1) | async-done | bytes 1572896 | tf_op jit(solution)/shard_map/all_to_all | solution.py:103
  246.4 14.1 %scatter_custom_fusion.2 = f32[1536,512]{1,0:T(8,128)} fusion(f32[1536,512]{1,0:T(8,128)} %copy.39, s32[1536]{0:T(1024)} %reshape.300, bf16[1536,512]{1,0:T(8,128)(2,1)} %bitcast.73), kind=kCustom, calls=%fused_computation.62 | custom fusion | flops 1572864 | bytes 4718592 | tf_op jit(solution)/shard_map/scatter-add | solution.py:104
  260.5 3.5 copy.40
  264.1 4.0 multiply_reduce_fusion.8
  270.7 3.2 fusion.131
  273.9 2.0 fusion.28
  278.7 2.5 fusion.26
  281.3 2.4 fusion.25
  285.1 3.1 fusion.23
  288.8 5.5 %fusion.113 = (f32[512]{0:T(512)S(1)}, f32[512]{0:T(512)S(1)}, f32[512]{0:T(512)S(1)}, bf16[1536,512]{0,1:T(8,128)(2,1)}) fusion(f32[1536]{0:T(1024)S(1)} %copy-done.62, f32[1536,512]{0,1:T(8,128)} %copy-done.8, f32[1536]{0:T(1024)S(1)} %copy-done.51, f32[1536]{0:T(1024)S(1)} %copy-done.64, f32[512]{0:T(512)S(1)} %bitcast.247, ...), kind=kLoop, calls=%fused_computation.251 | loop fusion | flops 17299968 | bytes 9488384 | tf_op jit(solution)/shard_map/reduce_sum | solution.py:41
  294.4 2.7 copy.43
  298.7 4.8 %fusion.133 = (f32[512]{0:T(512)S(1)}, bf16[2304,512]{1,0:T(8,128)(2,1)S(1)}) fusion(f32[2304,512]{1,0:T(8,128)} %copy-done.14, bf16[6,512,512]{2,1,0:T(8,128)(2,1)} %param.30, bf16[2304,512]{0,1:T(8,128)(2,1)S(1)} %copy-done.28), kind=kOutput, calls=%fused_computation.269 | convolution fusion | flops 1219755520 | bytes 9963520 | tf_op jit(solution)/shard_map/dot_general | solution.py:19
  304.0 2.3 reduce_sum.459
  306.5 24.0 %all-reduce = (f32[3,512]{1,0:T(4,128)}, f32[4,512]{1,0:T(4,128)}, f32[6,4,512]{2,1,0:T(4,128)}) all-reduce(f32[3,512]{1,0:T(4,128)S(1)} %convolution_bitcast_fusion.7, f32[4,512]{1,0:T(4,128)S(1)} %fusion.36, f32[6,4,512]{2,1,0:T(4,128)S(1)} %constant_dynamic-update-slice_fusion), channel_id=1, replica_groups=mesh['gp'=8] {'gp'}, use_global_device_ids=true, to_apply=%region_27.29 | all-reduce | flops 15872 | bytes 126976 | tf_op jit(solution)/shard_map/psum | solution.py:116
  330.5 1.8 fusion.40
  332.4 123.9 %all-reduce.4.cloned.1.call-done = (f32[272,512]{1,0:T(8,128)}, f32[1536,512]{1,0:T(8,128)}, f32[1024,512]{1,0:T(8,128)}, f32[512,512]{1,0:T(8,128)}, f32[6,512,512]{2,1,0:T(8,128)}) async-done(((f32[272,512]{1,0:T(8,128)}, f32[1536,512]{1,0:T(8,128)}, f32[1024,512]{1,0:T(8,128)}, f32[512,512]{1,0:T(8,128)}, f32[6,512,512]{2,1,0:T(8,128)}), (f32[272,512]{1,0:T(8,128)}, f32[1536,512]{1,0:T(8,128)}, ...) | async-done | bytes 13139984 | tf_op jit(solution)/shard_map/psum | solution.py:116
  456.3 2.0 copy.62
  458.3 4.0 copy.63
  465.3 2.7 copy.66
  (324 shorter events, 36.7 us)
Async XLA Ops:
  10.4 5.2 %copy-start.57 = (f32[1,1,512]{2,1,0:T(1,128)}, f32[1,1,512]{2,1,0:T(1,128)S(1)}, u32[]{:S(2)}) copy-start(f32[1,1,512]{2,1,0:T(1,128)S(1)} %get-tuple-element.94) | copy-start | bytes 6148
  10.4 5.2 %copy-start.71 = (f32[1,1,512]{2,1,0:T(1,128)}, f32[1,1,512]{2,1,0:T(1,128)S(1)}, u32[]{:S(2)}) copy-start(f32[1,1,512]{2,1,0:T(1,128)S(1)} %get-tuple-element.93) | copy-start | bytes 6148
  10.4 38.6 %copy-start.69 = (f32[1,1,512]{2,1,0:T(1,128)}, f32[1,1,512]{2,1,0:T(1,128)S(1)}, u32[]{:S(2)}) copy-start(f32[1,1,512]{2,1,0:T(1,128)S(1)} %get-tuple-element.82) | copy-start | bytes 6148
  25.6 7.6 %copy-start.52 = (s32[8,192]{1,0:T(8,128)S(1)}, s32[8,192]{1,0:T(8,128)}, u32[]{:S(2)}) copy-start(s32[8,192]{1,0:T(8,128)} %param.21) | copy-start | bytes 18436
  25.6 9.7 %copy-start.60 = (s32[2304]{0:T(1024)S(1)}, s32[2304]{0:T(1024)}, u32[]{:S(2)}) copy-start(s32[2304]{0:T(1024)} %param.22) | copy-start | bytes 27652
  25.6 9.7 %copy-start.59 = (s32[2304]{0:T(1024)S(1)}, s32[2304]{0:T(1024)}, u32[]{:S(2)}) copy-start(s32[2304]{0:T(1024)} %param.23) | copy-start | bytes 27652
  25.6 10.3 %copy-start.90 = (bf16[3,512]{1,0:T(4,128)(2,1)S(1)}, bf16[3,512]{1,0:T(4,128)(2,1)}, u32[]{:S(2)}) copy-start(bf16[3,512]{1,0:T(4,128)(2,1)} %param.25) | copy-start | bytes 9220
  25.6 10.3 %copy-start.92 = (bf16[128,3]{0,1:T(4,128)(2,1)S(1)}, bf16[128,3]{0,1:T(4,128)(2,1)}, u32[]{:S(2)}) copy-start(bf16[128,3]{0,1:T(4,128)(2,1)} %param.19) | copy-start | bytes 2308
  28.5 10.8 %copy-start.19 = (bf16[1024,512]{1,0:T(8,128)(2,1)S(1)}, bf16[1024,512]{1,0:T(8,128)(2,1)}, u32[]{:S(2)}) copy-start(bf16[1024,512]{1,0:T(8,128)(2,1)} %param.28) | copy-start | bytes 3145732
  28.5 54.6 %all-to-all-start = ((bf16[8,192,512]{2,1,0:T(8,128)(2,1)}), bf16[8,192,512]{2,1,0:T(8,128)(2,1)}, u32[]{:S(2)}, u32[]{:S(2)}) async-start(bf16[8,192,512]{2,1,0:T(8,128)(2,1)} %broadcast_select_fusion), calls=%async_computation | async-start | bytes 3145728 | tf_op jit(solution)/shard_map/all_to_all | solution.py:72
  35.2 6.7 %copy-start.67 = (f32[1,1,512]{2,1,0:T(1,128)}, f32[1,1,512]{2,1,0:T(1,128)S(1)}, u32[]{:S(2)}) copy-start(f32[1,1,512]{2,1,0:T(1,128)S(1)} %get-tuple-element.102) | copy-start | bytes 6148
  37.6 4.4 copy-start.37
  37.6 7.4 %copy-start.74 = (f32[128]{0:T(128)}, f32[128]{0:T(128)S(1)}, u32[]{:S(2)}) copy-start(f32[128]{0:T(128)S(1)} %broadcast_multiply_fusion.17) | copy-start | bytes 1540
  37.8 7.2 %copy-start.79 = (f32[128]{0:T(128)}, f32[128]{0:T(128)S(1)}, u32[]{:S(2)}) copy-start(f32[128]{0:T(128)S(1)} %add_rsqrt_fusion.5) | copy-start | bytes 1540
  42.0 11.6 %copy-start.5 = (bf16[1536,512]{0,1:T(8,128)(2,1)}, bf16[1536,512]{0,1:T(8,128)(2,1)S(1)}, u32[]{:S(2)}) copy-start(bf16[1536,512]{0,1:T(8,128)(2,1)S(1)} %copy.36) | copy-start | bytes 4718596
  48.1 5.4 %copy-start.55 = (f32[1536]{0:T(1024)}, f32[1536]{0:T(1024)S(1)}, u32[]{:S(2)}) copy-start(f32[1536]{0:T(1024)S(1)} %add_rsqrt_fusion.2) | copy-start | bytes 18436
  48.9 4.6 copy-start.61
  48.9 4.6 copy-start.63
  61.8 5.4 %copy-start.14 = (f32[2304,512]{1,0:T(8,128)}, f32[2304,512]{1,0:T(8,128)S(1)}, u32[]{:S(2)}) copy-start(f32[2304,512]{1,0:T(8,128)S(1)} %convolution_add_fusion.4) | copy-start | bytes 14155780
  83.0 14.9 %copy-start.11 = (bf16[2304,512]{0,1:T(8,128)(2,1)}, bf16[2304,512]{0,1:T(8,128)(2,1)S(1)}, u32[]{:S(2)}) copy-start(bf16[2304,512]{0,1:T(8,128)(2,1)S(1)} %add_convert_fusion.1) | copy-start | bytes 7077892
  88.0 9.9 %copy-start.78 = (pred[2304]{0:T(1024)(128)(4,1)S(1)}, pred[2304]{0:T(1024)(128)(4,1)}, u32[]{:S(2)}) copy-start(pred[2304]{0:T(1024)(128)(4,1)} %get-tuple-element.133) | copy-start | bytes 6916
  97.9 5.6 %copy-start.95 = (f32[1,1,512]{2,1,0:T(1,128)S(1)}, f32[1,1,512]{2,1,0:T(1,128)}, u32[]{:S(2)}) copy-start(f32[1,1,512]{2,1,0:T(1,128)} %get-tuple-element.91) | copy-start | bytes 6148
  103.5 5.6 %slice-start.2 = ((s8[4718592]{0:T(1024)(128)(4,1)}), s8[4194304]{0:T(1024)(128)(4,1)S(1)}, s32[]{:S(2)}) async-start(s8[4718592]{0:T(1024)(128)(4,1)} %bitcast.207), calls=%async_computation.5 | async-start | bytes 8388608
  103.5 5.6 %slice-start.3 = ((s8[4718592]{0:T(1024)(128)(4,1)}), s8[524288]{0:T(1024)(128)(4,1)S(1)}, s32[]{:S(2)}) async-start(s8[4718592]{0:T(1024)(128)(4,1)} %bitcast.207), calls=%async_computation.6 | async-start | bytes 1048576
  112.6 22.7 %copy-start.20 = (bf16[1024,512]{1,0:T(8,128)(2,1)S(1)}, bf16[1024,512]{1,0:T(8,128)(2,1)}, u32[]{:S(2)}) copy-start(bf16[1024,512]{1,0:T(8,128)(2,1)} %param.28) | copy-start | bytes 3145732
  112.6 22.8 %copy-start.34 = (f32[128,512]{1,0:T(8,128)S(1)}, f32[128,512]{1,0:T(8,128)}, u32[]{:S(2)}) copy-start(f32[128,512]{1,0:T(8,128)} %fusion.86) | copy-start | bytes 786436
  112.6 22.8 %copy-start.83 = (f32[1,1,512]{2,1,0:T(1,128)S(1)}, f32[1,1,512]{2,1,0:T(1,128)}, u32[]{:S(2)}) copy-start(f32[1,1,512]{2,1,0:T(1,128)} %get-tuple-element.88) | copy-start | bytes 6148
  112.6 23.0 %copy-start.94 = (f32[1,1,512]{2,1,0:T(1,128)S(1)}, f32[1,1,512]{2,1,0:T(1,128)}, u32[]{:S(2)}) copy-start(f32[1,1,512]{2,1,0:T(1,128)} %get-tuple-element.87) | copy-start | bytes 6148
  118.8 18.5 %copy-start.33 = (bf16[128,512]{1,0:T(8,128)(2,1)S(1)}, bf16[128,512]{1,0:T(8,128)(2,1)}, u32[]{:S(2)}) copy-start(bf16[128,512]{1,0:T(8,128)(2,1)} %param.32) | copy-start | bytes 393220
  118.8 18.5 %copy-start.66 = (f32[1,1,512]{2,1,0:T(1,128)S(1)}, f32[1,1,512]{2,1,0:T(1,128)}, u32[]{:S(2)}) copy-start(f32[1,1,512]{2,1,0:T(1,128)} %get-tuple-element.86) | copy-start | bytes 6148
  118.8 19.3 %copy-start.68 = (f32[1,1,512]{2,1,0:T(1,128)S(1)}, f32[1,1,512]{2,1,0:T(1,128)}, u32[]{:S(2)}) copy-start(f32[1,1,512]{2,1,0:T(1,128)} %copy-done.67) | copy-start | bytes 6148
  118.8 19.3 %copy-start.75 = (f32[128]{0:T(128)S(1)}, f32[128]{0:T(128)}, u32[]{:S(2)}) copy-start(f32[128]{0:T(128)} %copy-done.74) | copy-start | bytes 1540
  118.8 19.3 %copy-start.80 = (f32[128]{0:T(128)S(1)}, f32[128]{0:T(128)}, u32[]{:S(2)}) copy-start(f32[128]{0:T(128)} %copy-done.79) | copy-start | bytes 1540
  118.8 19.3 %copy-start.82 = (f32[1,1,512]{2,1,0:T(1,128)S(1)}, f32[1,1,512]{2,1,0:T(1,128)}, u32[]{:S(2)}) copy-start(f32[1,1,512]{2,1,0:T(1,128)} %get-tuple-element.85) | copy-start | bytes 6148
  135.6 7.0 %copy-start.41 = (f32[128,512]{1,0:T(8,128)}, f32[128,512]{1,0:T(8,128)S(1)}, u32[]{:S(2)}) copy-start(f32[128,512]{1,0:T(8,128)S(1)} %fusion.33) | copy-start | bytes 786436
  138.1 6.1 %copy-start.23 = (bf16[128,512]{1,0:T(8,128)(2,1)S(1)}, bf16[128,512]{1,0:T(8,128)(2,1)}, u32[]{:S(2)}) copy-start(bf16[128,512]{1,0:T(8,128)(2,1)} %copy-done.22) | copy-start | bytes 393220
  152.5 12.9 %slice-start = ((s8[4718592]{0:T(1024)(128)(4,1)}), s8[524288]{0:T(1024)(128)(4,1)S(1)}, s32[]{:S(2)}) async-start(s8[4718592]{0:T(1024)(128)(4,1)} %bitcast.205), calls=%async_computation.3 | async-start | bytes 1048576
  158.7 6.7 %slice-start.1 = ((s8[4718592]{0:T(1024)(128)(4,1)}), s8[4194304]{0:T(1024)(128)(4,1)S(1)}, s32[]{:S(2)}) async-start(s8[4718592]{0:T(1024)(128)(4,1)} %bitcast.205), calls=%async_computation.4 | async-start | bytes 8388608
  158.7 6.7 %copy-start.4 = (f32[2304,512]{0,1:T(8,128)S(1)}, f32[2304,512]{0,1:T(8,128)}, u32[]{:S(2)}) copy-start(f32[2304,512]{0,1:T(8,128)} %copy.38) | copy-start | bytes 14155780
  158.7 8.7 %slice-start.12 = ((s8[4718592]{0:T(1024)(128)(4,1)}), s8[4194304]{0:T(1024)(128)(4,1)S(1)}, s32[]{:S(2)}) async-start(s8[4718592]{0:T(1024)(128)(4,1)} %bitcast.219), calls=%async_computation.15 | async-start | bytes 8388608
  165.4 6.6 %slice-start.4 = ((s8[4718592]{0:T(1024)(128)(4,1)}), s8[524288]{0:T(1024)(128)(4,1)S(1)}, s32[]{:S(2)}) async-start(s8[4718592]{0:T(1024)(128)(4,1)} %bitcast.209), calls=%async_computation.7 | async-start | bytes 1048576
  167.4 4.7 copy-start.25
  167.4 4.7 slice-start.5
  213.2 4.5 copy-start.10
  213.2 4.5 copy-start.18
  222.3 24.0 %all-to-all-start.1 = ((bf16[8,192,512]{2,1,0:T(8,128)(2,1)}), bf16[8,192,512]{2,1,0:T(8,128)(2,1)}, u32[]{:S(2)}, u32[]{:S(2)}) async-start(bf16[8,192,512]{2,1,0:T(8,128)(2,1)} %bitcast.216), calls=%async_computation.1 | async-start | bytes 3145728 | tf_op jit(solution)/shard_map/all_to_all | solution.py:103
  225.4 230.9 %all-reduce.4.cloned.1.call-start = ((), (), s32[]{:S(2)}) async-start(), calls=%async_computation.2 | async-start | bytes 26279936 | tf_op jit(solution)/shard_map/psum | solution.py:116
  225.4 5.1 %copy-start.12 = (bf16[2304,512]{0,1:T(8,128)(2,1)S(1)}, bf16[2304,512]{0,1:T(8,128)(2,1)}, u32[]{:S(2)}) copy-start(bf16[2304,512]{0,1:T(8,128)(2,1)} %copy-done.11) | copy-start | bytes 7077892
  227.4 8.2 %slice-start.6 = ((s8[4718592]{0:T(1024)(128)(4,1)}), s8[4194304]{0:T(1024)(128)(4,1)S(1)}, s32[]{:S(2)}) async-start(s8[4718592]{0:T(1024)(128)(4,1)} %bitcast.211), calls=%async_computation.9 | async-start | bytes 8388608
  227.4 8.2 %slice-start.16 = ((s8[4718592]{0:T(1024)(128)(4,1)}), s8[4194304]{0:T(1024)(128)(4,1)S(1)}, s32[]{:S(2)}) async-start(s8[4718592]{0:T(1024)(128)(4,1)} %bitcast.223), calls=%async_computation.19 | async-start | bytes 8388608
  230.6 5.1 %slice-start.7 = ((s8[4718592]{0:T(1024)(128)(4,1)}), s8[524288]{0:T(1024)(128)(4,1)S(1)}, s32[]{:S(2)}) async-start(s8[4718592]{0:T(1024)(128)(4,1)} %bitcast.211), calls=%async_computation.10 | async-start | bytes 1048576
  230.6 5.1 %slice-start.17 = ((s8[4718592]{0:T(1024)(128)(4,1)}), s8[524288]{0:T(1024)(128)(4,1)S(1)}, s32[]{:S(2)}) async-start(s8[4718592]{0:T(1024)(128)(4,1)} %bitcast.223), calls=%async_computation.20 | async-start | bytes 1048576
  237.3 41.4 %copy-start.27 = (bf16[2304,512]{0,1:T(8,128)(2,1)}, bf16[2304,512]{0,1:T(8,128)(2,1)S(1)}, u32[]{:S(2)}) copy-start(bf16[2304,512]{0,1:T(8,128)(2,1)S(1)} %get-tuple-element.71) | copy-start | bytes 7077892
  264.1 4.7 copy-start.7
  270.7 8.0 %slice-start.10 = ((s8[4718592]{0:T(1024)(128)(4,1)}), s8[4194304]{0:T(1024)(128)(4,1)S(1)}, s32[]{:S(2)}) async-start(s8[4718592]{0:T(1024)(128)(4,1)} %bitcast.217), calls=%async_computation.13 | async-start | bytes 8388608
  273.9 4.8 %slice-start.11 = ((s8[4718592]{0:T(1024)(128)(4,1)}), s8[524288]{0:T(1024)(128)(4,1)S(1)}, s32[]{:S(2)}) async-start(s8[4718592]{0:T(1024)(128)(4,1)} %bitcast.217), calls=%async_computation.14 | async-start | bytes 1048576
  275.9 5.2 %slice-start.14 = ((s8[4718592]{0:T(1024)(128)(4,1)}), s8[4194304]{0:T(1024)(128)(4,1)S(1)}, s32[]{:S(2)}) async-start(s8[4718592]{0:T(1024)(128)(4,1)} %bitcast.221), calls=%async_computation.17 | async-start | bytes 8388608
  294.3 4.3 copy-start.28
  298.7 4.9 %copy-start.54 = (bf16[2304,4]{0,1:T(4,128)(2,1)S(1)}, bf16[2304,4]{0,1:T(4,128)(2,1)}, u32[]{:S(2)}) copy-start(bf16[2304,4]{0,1:T(4,128)(2,1)} %param.20) | copy-start | bytes 55300
  303.6 26.9 %copy-start.32 = (bf16[1536,512]{1,0:T(8,128)(2,1)S(1)}, bf16[1536,512]{1,0:T(8,128)(2,1)}, u32[]{:S(2)}) copy-start(bf16[1536,512]{1,0:T(8,128)(2,1)} %copy-done.31) | copy-start | bytes 4718596
  303.6 26.9 %copy-start.40 = (bf16[272,512]{1,0:T(8,128)(2,1)S(1)}, bf16[272,512]{1,0:T(8,128)(2,1)}, u32[]{:S(2)}) copy-start(bf16[272,512]{1,0:T(8,128)(2,1)} %param.24) | copy-start | bytes 835588
  456.3 6.1 %copy-start.30 = (f32[1024,512]{1,0:T(8,128)S(1)}, f32[1024,512]{1,0:T(8,128)}, u32[]{:S(2)}) copy-start(f32[1024,512]{1,0:T(8,128)} %get-tuple-element.162) | copy-start | bytes 6291460
  456.3 9.0 %slice-start.8 = ((s8[6291456]{0:T(1024)(128)(4,1)}), s8[4194304]{0:T(1024)(128)(4,1)S(1)}, s32[]{:S(2)}) async-start(s8[6291456]{0:T(1024)(128)(4,1)} %bitcast.213), calls=%async_computation.11 | async-start | bytes 8388608
  458.3 7.0 %slice-start.9 = ((s8[6291456]{0:T(1024)(128)(4,1)}), s8[2097152]{0:T(1024)(128)(4,1)S(1)}, s32[]{:S(2)}) async-start(s8[6291456]{0:T(1024)(128)(4,1)} %bitcast.213), calls=%async_computation.12 | async-start | bytes 4194304
  (61 other events, 163.6 us)
Sparse Core Ops, SparseCore 0:
  288.3 167.9 all-reduce.3
where the time goes:
time: 480 us; the launch traced here: 475 us
  waiting for transfers between devices  133 us (28%)
  other arithmetic  118 us (25%)
  matrix products  97.6 us (20%)
  local copies, waits for them, and re-layouts  79.3 us (17%)
  blocking collectives  24 us (5%)
  between operations  15.7 us (3%)
  starting transfers between devices  7.75 us (2%)
    psum x1, waiting for transfers between devices, local_step(): weight_grads = lax.psum(weight_grads, AXIS_NAME)  124 us
    dot_general x15, matrix products, matmul(): return jnp.dot(lhs, rhs, preferred_element_type=jnp.float32)  36 us
    dot_general x13, matrix products, contract_cols(): lax.dot_general(lhs, rhs, (((1,), (1,)), ((), ())), preferred_element_typ...  35.3 us
    dot_general x15, matrix products, contract_rows(): lax.dot_general(lhs, rhs, (((0,), (0,)), ((), ())), preferred_element_typ...  26.2 us
    psum x1, blocking collectives, local_step(): weight_grads = lax.psum(weight_grads, AXIS_NAME)  24 us
    unnamed x251, local copies, waits for them, and re-layouts  24 us
    scatter-add x1, other arithmetic, local_step(): jax.ops.segment_sum(d_pre3_wide, edge_src, num_segments=slot_rows)  18 us
    scatter-add x1, other arithmetic, local_step(): jax.ops.segment_sum(d_pre3_wide, edge_dst, num_segments=mesh_rows)  17.1 us
  transfers between devices with their start and end apart: 3, of which 2 were waited for; matrix products, arithmetic and copies ran while one was open for 16% of the time, Pallas kernels for 0%

commit v1 on v0

v1 whole, which is shorter than its diff:
```python
import jax
import jax.numpy as jnp
from jax import lax
from jax.experimental import pallas as pl
from jax.experimental.pallas import tpu as pltpu
from jax.sharding import PartitionSpec as P

LN_EPS = 1e-5
AXIS_NAME = 'gp'
MESH_ID = pl.DeviceIdType.MESH
BF = jnp.bfloat16
F32 = jnp.float32


def chunked(rows, step, fn):
    lax.fori_loop(0, rows // step, lambda i, c: (fn(i * step), c)[1], 0)


def row_slice(start, size):
    return pl.ds(pl.multiple_of(start, 16), size)


def place():
    me = lax.axis_index(AXIS_NAME)
    core, xpos, ypos = me % 2, (me // 2) % 2, me // 4
    return me, core, xpos, ypos, me + 1 - 2 * core, me + 2 - 4 * xpos, me + 4 - 8 * ypos


def remote(src, dst, sems, idx, dev):
    return pltpu.make_async_remote_copy(src_ref=src, dst_ref=dst, send_sem=sems.at[0, idx], recv_sem=sems.at[1, idx],
                                        device_id=(dev,), device_id_type=MESH_ID)


def barrier_signal():
    me = lax.axis_index(AXIS_NAME)
    barrier = pltpu.get_barrier_semaphore()
    for step in range(1, 8):
        pl.semaphore_signal(barrier, inc=1, device_id=((me + step) % 8,), device_id_type=MESH_ID)


def barrier_wait():
    pl.semaphore_wait(pltpu.get_barrier_semaphore(), 7)


def flip(me, k):
    core, xpos, ypos = me % 2, (me // 2) % 2, me // 4
    core = 1 - core if k & 1 else core
    xpos = 1 - xpos if k & 2 else xpos
    ypos = 1 - ypos if k & 4 else ypos
    return core + 2 * xpos + 4 * ypos


NUM_SEMS = 10


def reduce_steps(grad, out, half_in, mid, last, sems):
    rows = grad.shape[0]
    r2, r4, r8, r16 = rows // 2, rows // 4, rows // 8, rows // 16
    _, core, xpos, ypos, pc, px, py = place()
    sent = []

    def go(src, dst, idx, dev):
        copy = remote(src, dst, sems, idx, dev)
        copy.start()
        sent.append(copy)
        return copy

    first = go(grad.at[row_slice((1 - core) * r2, r2)], half_in, 0, pc)
    yield
    first.wait_recv()
    base = core * r2

    def chip_sum(off):
        return grad[row_slice(base + off, 16), :] + half_in[row_slice(off, 16), :]

    away_a, away_b = (1 - xpos) * r8, r4 + (1 - ypos) * r8
    keep_a, keep_b = xpos * r8, r4 + ypos * r8

    def send_mid(i):
        mid[0, row_slice(i, 16), :] = chip_sum(away_a + i).astype(BF)
        mid[1, row_slice(i, 16), :] = chip_sum(away_b + i).astype(BF)
    chunked(r8, 16, send_mid)
    c_a = go(mid.at[0], mid.at[2], 1, px)
    c_b = go(mid.at[1], mid.at[3], 2, py)
    yield
    c_a.wait_recv()
    c_b.wait_recv()

    def two_sum(which, keep, off):
        return chip_sum(keep + off) + mid[2 + which, row_slice(off, 16), :].astype(F32)

    def send_last(i):
        last[0, row_slice(i, 16), :] = two_sum(0, keep_a, (1 - ypos) * r16 + i).astype(BF)
        last[1, row_slice(i, 16), :] = two_sum(1, keep_b, (1 - xpos) * r16 + i).astype(BF)
    chunked(r16, 16, send_last)
    c_a = go(last.at[0], last.at[2], 3, py)
    c_b = go(last.at[1], last.at[3], 4, px)
    yield
    c_a.wait_recv()
    c_b.wait_recv()
    pos_a, pos_b = base + keep_a + ypos * r16, base + keep_b + xpos * r16

    def total(i):
        out[row_slice(pos_a + i, 16), :] = (two_sum(0, keep_a, ypos * r16 + i) + last[2, row_slice(i, 16), :].astype(F32)).astype(BF)
        out[row_slice(pos_b + i, 16), :] = (two_sum(1, keep_b, xpos * r16 + i) + last[3, row_slice(i, 16), :].astype(F32)).astype(BF)
    chunked(r16, 16, total)
    sl_a, sl_b = out.at[row_slice(pos_a, r16)], out.at[row_slice(pos_b, r16)]
    c_a = go(sl_a, sl_a, 5, py)
    c_b = go(sl_b, sl_b, 6, px)
    yield
    c_a.wait_recv()
    c_b.wait_recv()
    sl_a, sl_b = out.at[row_slice(base + keep_a, r8)], out.at[row_slice(base + keep_b, r8)]
    c_a = go(sl_a, sl_a, 7, px)
    c_b = go(sl_b, sl_b, 8, py)
    yield
    c_a.wait_recv()
    c_b.wait_recv()
    sl = out.at[row_slice(base, r2)]
    c_c = go(sl, sl, 9, pc)
    yield
    c_c.wait_recv()
    for copy in sent:
        copy.wait_send()


def dot(lhs, rhs):
    return jnp.dot(lhs, rhs, preferred_element_type=F32)


def dot_rows(lhs, rhs):
    return lax.dot_general(lhs, rhs, (((0,), (0,)), ((), ())), preferred_element_type=F32)


def dot_cols(lhs, rhs):
    return lax.dot_general(lhs, rhs, (((1,), (1,)), ((), ())), preferred_element_type=F32)


def sigmoid(val):
    return 0.5 * jnp.tanh(0.5 * val) + 0.5


def pick(idx_col, size):
    ids = lax.broadcasted_iota(jnp.int32, (idx_col.shape[0], size), 1)
    return jnp.where(idx_col == ids, 1.0, 0.0).astype(BF)


def pick_t(idx_row, start, size):
    ids = lax.broadcasted_iota(jnp.int32, (size, idx_row.shape[1]), 0) + start
    return jnp.where(idx_row == ids, 1.0, 0.0).astype(BF)


def normalise(hidden, w_two, bias_two):
    out_lin = dot(hidden, w_two) + bias_two
    centered = out_lin - jnp.mean(out_lin, axis=-1, keepdims=True)
    inv_std = lax.rsqrt(jnp.mean(centered * centered, axis=-1, keepdims=True) + LN_EPS)
    return centered * inv_std, inv_std


def fold8(val):
    return jnp.sum(val.reshape(val.shape[0] // 8, 8, val.shape[1]), axis=0)


def layer_back(pre, sig, hidden, normed, inv_std, w_two, gamma, d_out, two_acc, vec_acc):
    d_normed = d_out * gamma
    d_lin = inv_std * (d_normed - jnp.mean(d_normed, axis=-1, keepdims=True)
                       - normed * jnp.mean(d_normed * normed, axis=-1, keepdims=True))
    d_lin_bf = d_lin.astype(BF)
    two_acc[...] += dot_rows(hidden, d_lin_bf)
    d_pre = dot_cols(d_lin_bf, w_two) * (sig * (1.0 + pre * (1.0 - sig)))
    vec_acc[0] += fold8(d_pre)
    vec_acc[1] += fold8(d_lin)
    vec_acc[2] += fold8(d_out * normed)
    vec_acc[3] += fold8(d_out)
    return d_pre.astype(BF)


def vec_block(vec_acc):
    rows = lax.broadcasted_iota(jnp.int32, (8, vec_acc.shape[2]), 0)
    out = jnp.zeros((8, vec_acc.shape[2]), F32)
    for j in range(4):
        out = jnp.where(rows == j, jnp.sum(vec_acc[j], axis=0, keepdims=True), out)
    return out


def tiles(first, last, tile, fn):
    def step(i, carry):
        fn(pl.multiple_of(i * tile, tile))
        return carry
    lax.fori_loop(first, last, step, 0)


TILE = 256
SLOTS = 192


def encode_body(grid_in, mesh_static, edge_static, send_col, w_grid_in, w_mesh_in, w_edge_in, w_grid_up, w_two, vec, d_grid_out,
                incoming, edge_lat, mesh_lat, grid_out, d_grid_part, grad_a, vec5,
                grid_lat, outgoing, vec_acc, sems):
    me = lax.axis_index(AXIS_NAME)
    barrier_signal()

    def embed(x_val, w_in, k):
        pre = dot(x_val, w_in[...]) + vec[k, 0:1, :]
        hidden = (pre * sigmoid(pre)).astype(BF)
        normed, _ = normalise(hidden, w_two[k], vec[k, 1:2, :])
        return (normed * vec[k, 2:3, :] + vec[k, 3:4, :]).astype(BF)

    def grid_tile(row):
        grid_lat[pl.ds(row, TILE), :] = embed(grid_in[pl.ds(row, TILE), :], w_grid_in, 0)
    tiles(0, grid_in.shape[0] // TILE, TILE, grid_tile)

    barrier_wait()
    copies = []
    for k in (6, 7, 2, 3, 4, 5, 1, 0):
        peer = flip(me, k)
        there = pl.ds(pl.multiple_of(peer * SLOTS, SLOTS), SLOTS)
        here = pl.ds(pl.multiple_of(me * SLOTS, SLOTS), SLOTS)
        rows = dot(pick(send_col[there, :], grid_lat.shape[0]), grid_lat[...]).astype(BF)
        if k == 0:
            incoming[here, :] = rows
        else:
            outgoing[there, :] = rows
            copy = remote(outgoing.at[there], incoming.at[here], sems, k, peer)
            copy.start()
            copies.append(copy)

    def edge_tile(row):
        edge_lat[pl.ds(row, TILE), :] = embed(edge_static[pl.ds(row, TILE), :], w_edge_in, 2)
    tiles(0, edge_static.shape[0] // TILE, TILE, edge_tile)
    mesh_lat[...] = embed(mesh_static[...], w_mesh_in, 1)

    grad_a[...] = jnp.zeros_like(grad_a)
    vec_acc[...] = jnp.zeros_like(vec_acc)
    two_acc, up_acc = grad_a.at[0:512], grad_a.at[512:1024]

    def cell_tile(row):
        lat = grid_lat[pl.ds(row, TILE), :]
        pre = dot(lat, w_grid_up[...]) + vec[5, 0:1, :]
        sig = sigmoid(pre)
        hidden = (pre * sig).astype(BF)
        normed, inv_std = normalise(hidden, w_two[5], vec[5, 1:2, :])
        upd = normed * vec[5, 2:3, :] + vec[5, 3:4, :]
        grid_out[pl.ds(row, TILE), :] = (lat.astype(F32) + upd).astype(BF)
        d_top = d_grid_out[pl.ds(row, TILE), :].astype(F32)
        d_pre = layer_back(pre, sig, hidden, normed, inv_std, w_two[5], vec[5, 2:3, :], d_top, two_acc, vec_acc)
        up_acc[...] += dot_rows(lat, d_pre)
        d_grid_part[pl.ds(row, TILE), :] = d_top + dot_cols(d_pre, w_grid_up[...])
    tiles(0, grid_in.shape[0] // TILE, TILE, cell_tile)
    vec5[...] = vec_block(vec_acc)
    for copy in copies:
        copy.wait()


def update_body(incoming, edge_lat, mesh_lat, idx_col, src_row, dst_row, send_row, edge_static, edge_static_t, mesh_static, mesh_static_t, grid_in,
                w_grid_in, w_mesh_in, w_edge_in, w_edge_up, w_mesh_up, w_two, vec, d_mesh_out, d_grid_part, grad_a, vec5,
                mesh_out, d_grid_in, sum_a, sum_b, sum_c, sum_e, sum_d,
                pre3, normed3, inv3, d_pre3, d_slot, d_incoming, d_outgoing, agg, d_node, d_mesh, d_agg, vec_acc,
                grad_b, grad_c, half_a, half_b, mid_a, mid_b, mid_c, mid_e, mid_d, last_a, last_b, last_c, last_e, last_d,
                sem_a, sem_b, sem_c, sem_e, sem_d, sems):
    me = lax.axis_index(AXIS_NAME)
    n_edge, n_grid, n_mesh, n_slot = edge_lat.shape[0], grid_in.shape[0], mesh_lat.shape[0], incoming.shape[0]
    grad_e, grad_d = normed3.at[0:1024], normed3.at[1024:2048]
    half_c, half_e, half_d = pre3.at[0:1024], pre3.at[1024:1536], pre3.at[1536:2048]
    up_edge, up_send, up_recv = w_edge_up.at[0:512], w_edge_up.at[512:1024], w_edge_up.at[1024:1536]
    node_self, node_agg = w_mesh_up.at[0:512], w_mesh_up.at[512:1024]
    live = []

    def advance():
        for gen in list(live):
            try:
                next(gen)
            except StopIteration:
                live.remove(gen)

    def begin(*args):
        gen = reduce_steps(*args)
        next(gen)
        live.append(gen)

    def groups(count, fn):
        for g in range(3):
            tiles(g * count // 3, (g + 1) * count // 3, TILE, fn)
            advance()

    barrier_signal()
    barrier_wait()
    begin(grad_a, sum_a, half_a, mid_a, last_a, sem_a)
    agg[...] = jnp.zeros_like(agg)

    def edge_forward(row):
        here = pl.ds(row, TILE)
        lat = edge_lat[here, :]
        sender = dot(pick(idx_col[here, 0:1], n_slot), incoming[...]).astype(BF)
        receiver = dot(pick(idx_col[here, 1:2], n_mesh), mesh_lat[...]).astype(BF)
        pre = dot(jnp.concatenate([lat, sender, receiver], axis=1), w_edge_up[...]) + vec[3, 0:1, :]
        hidden = (pre * sigmoid(pre)).astype(BF)
        normed, inv_std = normalise(hidden, w_two[3], vec[3, 1:2, :])
        pre3[here, :] = pre
        normed3[here, :] = normed
        inv3[here, :] = inv_std
        edge_new = (lat.astype(F32) + normed * vec[3, 2:3, :] + vec[3, 3:4, :]).astype(BF)
        agg[...] += dot(pick_t(dst_row[:, here], 0, n_mesh), edge_new)
    groups(n_edge // TILE, edge_forward)

    def clear_vec():
        vec_acc[...] = jnp.zeros_like(vec_acc)

    grad_b[...] = jnp.zeros_like(grad_b)
    clear_vec()
    lat = mesh_lat[...]
    agg_bf = agg[...].astype(BF)
    pre = dot(jnp.concatenate([lat, agg_bf], axis=1), w_mesh_up[...]) + vec[4, 0:1, :]
    sig = sigmoid(pre)
    hidden = (pre * sig).astype(BF)
    normed, inv_std = normalise(hidden, w_two[4], vec[4, 1:2, :])
    mesh_out[...] = (lat.astype(F32) + normed * vec[4, 2:3, :] + vec[4, 3:4, :]).astype(BF)
    d_top = d_mesh_out[...].astype(F32)
    d_pre = layer_back(pre, sig, hidden, normed, inv_std, w_two[4], vec[4, 2:3, :], d_top, grad_b.at[1024:1536], vec_acc)
    grad_b[0:512, :] = dot_rows(lat, d_pre)
    grad_b[512:1024, :] = dot_rows(agg_bf, d_pre)
    d_mesh[...] = d_top + dot_cols(d_pre, node_self[...])
    d_agg[...] = dot_cols(d_pre, node_agg[...]).astype(BF)
    vec4 = vec_block(vec_acc)
    advance()
    begin(grad_b, sum_b, half_b, mid_b, last_b, sem_b)

    clear_vec()
    d_node[...] = jnp.zeros_like(d_node)
    grad_c[...] = jnp.zeros_like(grad_c)

    def edge_backward(row):
        here = pl.ds(row, TILE)
        d_out = dot(pick(idx_col[here, 1:2], n_mesh), d_agg[...])
        pre = pre3[here, :]
        sig = sigmoid(pre)
        hidden = (pre * sig).astype(BF)
        d_pre = layer_back(pre, sig, hidden, normed3[here, :], inv3[here, :], w_two[3], vec[3, 2:3, :], d_out, grad_c.at[1536:2048], vec_acc)
        d_pre3[here, :] = d_pre
        d_node[...] += dot(pick_t(dst_row[:, here], 0, n_mesh), d_pre)
        grad_c[0:512, :] += dot_rows(edge_lat[here, :], d_pre)
    groups(n_edge // TILE, edge_backward)
    vec3 = vec_block(vec_acc)

    copies = []
    for k in (1, 6, 7, 2, 3, 4, 5, 0):
        peer = flip(me, k)
        start = pl.multiple_of(peer * SLOTS, SLOTS)
        there, here = pl.ds(start, SLOTS), pl.ds(pl.multiple_of(me * SLOTS, SLOTS), SLOTS)
        slot = dot(pick_t(src_row[...], start, SLOTS), d_pre3[...]).astype(BF)
        d_slot[there, :] = slot
        back = dot_cols(slot, up_send[...]).astype(BF)
        if k == 0:
            d_outgoing[here, :] = back
        else:
            d_incoming[there, :] = back
            copy = remote(d_incoming.at[there], d_outgoing.at[here], sems, k, peer)
            copy.start()
            copies.append(copy)
    advance()

    def slot_tile(row):
        here = pl.ds(row, TILE)
        grad_c[512:1024, :] += dot_rows(incoming[here, :], d_slot[here, :])
    tiles(0, n_slot // TILE, TILE, slot_tile)
    d_node_bf = d_node[...].astype(BF)
    grad_c[1024:1536, :] = dot_rows(lat, d_node_bf)
    d_mesh_full = d_mesh[...] + dot_cols(d_node_bf, up_recv[...])
    copies[0].wait_recv()
    begin(grad_c, sum_c, half_c, mid_c, last_c, sem_c)

    grad_e[...] = jnp.zeros_like(grad_e)
    grad_d[...] = jnp.zeros_like(grad_d)

    def recompute(x_val, w_in, k):
        pre = dot(x_val, w_in[...]) + vec[k, 0:1, :]
        sig = sigmoid(pre)
        hidden = (pre * sig).astype(BF)
        normed, inv_std = normalise(hidden, w_two[k], vec[k, 1:2, :])
        return pre, sig, hidden, normed, inv_std, w_two[k], vec[k, 2:3, :]

    clear_vec()
    d_pre = layer_back(*recompute(mesh_static[...], w_mesh_in, 1), d_mesh_full, grad_e.at[512:1024], vec_acc)
    grad_d[832:840, :] = dot(mesh_static_t[...], d_pre)[0:8, :]
    grad_d[792:800, :] = vec_block(vec_acc)
    clear_vec()

    def edge_embed_back(row):
        here = pl.ds(row, TILE)
        d_out = dot(pick(idx_col[here, 1:2], n_mesh), d_agg[...]) + dot_cols(d_pre3[here, :], up_edge[...])
        d_pre = layer_back(*recompute(edge_static[here, :], w_edge_in, 2), d_out, grad_e.at[0:512], vec_acc)
        grad_d[840:848, :] += dot(edge_static_t[:, here], d_pre)[0:8, :]
    groups(n_edge // TILE, edge_embed_back)
    grad_d[800:808, :] = vec_block(vec_acc)
    grad_d[808:816, :] = vec3
    grad_d[816:824, :] = vec4
    grad_d[824:832, :] = vec5[...]
    begin(grad_e, sum_e, half_e, mid_e, last_e, sem_e)

    for copy in copies[1:]:
        copy.wait_recv()
    clear_vec()

    def grid_back(row):
        here = pl.ds(row, TILE)
        x_val = grid_in[here, :]
        d_out = d_grid_part[here, :] + dot(pick_t(send_row[...], row, TILE), d_outgoing[...])
        d_pre = layer_back(*recompute(x_val, w_grid_in, 0), d_out, grad_d.at[0:512], vec_acc)
        grad_d[512:784, :] += dot_rows(x_val, d_pre)
        d_grid_in[here, :] = dot_cols(d_pre, w_grid_in[...])
    groups(n_grid // TILE, grid_back)
    grad_d[784:792, :] = vec_block(vec_acc)
    begin(grad_d, sum_d, half_d, mid_d, last_d, sem_d)
    while live:
        advance()
    for copy in copies:
        copy.wait_send()


def shape(rows, cols, dtype):
    return jax.ShapeDtypeStruct((rows, cols), dtype)


def solution(mesh):
    row_spec = P(AXIS_NAME, None)
    edge_spec = P(AXIS_NAME)
    rep_spec = P()
    in_specs = (row_spec, row_spec, row_spec, row_spec, edge_spec, edge_spec) + (rep_spec,) * 8 + (row_spec, row_spec)
    out_specs = (row_spec, row_spec, row_spec) + (rep_spec,) * 8
    vm = pl.BlockSpec(memory_space=pltpu.VMEM)

    def local_step(grid_in, mesh_static, edge_static, send_rows, edge_src, edge_dst, w_grid_in, w_mesh_in, w_edge_in, w_edge_up, w_mesh_up, w_grid_up, w_second, vectors, d_mesh_out, d_grid_out):
        latent = w_grid_up.shape[0]
        n_grid, n_mesh, n_edge, n_slot = grid_in.shape[0], mesh_static.shape[0], edge_src.shape[0], send_rows.size
        f_dim, m_dim, e_dim = w_grid_in.shape[0], w_mesh_in.shape[0], w_edge_in.shape[0]
        idx_col = jnp.stack([edge_src, edge_dst], axis=1)
        send_flat = send_rows.reshape(-1)

        def call(body, ins, outs, scratch, name, ident):
            return pl.pallas_call(
                body, out_shape=outs, in_specs=[vm] * len(ins), out_specs=[vm] * len(outs), scratch_shapes=scratch, name=name,
                compiler_params=pltpu.CompilerParams(collective_id=ident, has_side_effects=True, vmem_limit_bytes=67043328),
            )(*ins)

        incoming, edge_lat, mesh_lat, grid_out, d_grid_part, grad_a, vec5 = call(
            encode_body,
            (grid_in, mesh_static, edge_static, send_flat[:, None], w_grid_in, w_mesh_in, w_edge_in, w_grid_up, w_second, vectors, d_grid_out),
            [shape(n_slot, latent, BF), shape(n_edge, latent, BF), shape(n_mesh, latent, BF), shape(n_grid, latent, BF),
             shape(n_grid, latent, F32), shape(1024, latent, F32), shape(8, latent, F32)],
            [pltpu.VMEM((n_grid, latent), BF), pltpu.VMEM((n_slot, latent), BF), pltpu.VMEM((4, 8, latent), F32), pltpu.SemaphoreType.DMA((2, 8))],
            'encode', 0)

        r_a, r_b, r_c, r_e, r_d = 1024, 1536, 2048, 1024, 1024
        vmem = lambda rows, dtype: pltpu.VMEM((rows, latent), dtype)
        scratch = [vmem(n_edge, F32), vmem(n_edge, F32), pltpu.VMEM((n_edge, 1), F32), vmem(n_edge, BF), vmem(n_slot, BF), vmem(n_slot, BF), vmem(n_slot, BF),
                   vmem(n_mesh, F32), vmem(n_mesh, F32), vmem(n_mesh, F32), vmem(n_mesh, BF), pltpu.VMEM((4, 8, latent), F32),
                   vmem(r_b, F32), vmem(r_c, F32), vmem(r_a // 2, F32), vmem(r_b // 2, F32)]
        scratch += [pltpu.VMEM((4, r // 8, latent), BF) for r in (r_a, r_b, r_c, r_e, r_d)]
        scratch += [pltpu.VMEM((4, r // 16, latent), BF) for r in (r_a, r_b, r_c, r_e, r_d)]
        scratch += [pltpu.SemaphoreType.DMA((2, 10))] * 5 + [pltpu.SemaphoreType.DMA((2, 8))]
        pad_t = lambda val: jnp.pad(val.T, ((0, 16 - val.shape[1]), (0, 0)))
        mesh_out, d_grid_in, s_a, s_b, s_c, s_e, s_d = call(
            update_body,
            (incoming, edge_lat, mesh_lat, idx_col, edge_src[None, :], edge_dst[None, :], send_flat[None, :], edge_static, pad_t(edge_static),
             mesh_static, pad_t(mesh_static), grid_in, w_grid_in, w_mesh_in, w_edge_in, w_edge_up, w_mesh_up, w_second, vectors,
             d_mesh_out, d_grid_part, grad_a, vec5),
            [shape(n_mesh, latent, BF), shape(n_grid, f_dim, F32)] + [shape(r, latent, BF) for r in (r_a, r_b, r_c, r_e, r_d)],
            scratch, 'update', 1)

        o_v = latent + f_dim
        two = jnp.stack([s_d[:latent], s_e[latent:], s_e[:latent], s_c[3 * latent:], s_b[2 * latent:], s_a[:latent]]).astype(F32)
        vec = s_d[o_v:o_v + 48].reshape(6, 8, latent)[:, :4].astype(F32)
        return (mesh_out, grid_out, d_grid_in, s_d[latent:o_v].astype(F32), s_d[o_v + 48:o_v + 48 + m_dim].astype(F32),
                s_d[o_v + 56:o_v + 56 + e_dim].astype(F32), s_c[:3 * latent].astype(F32), s_b[:2 * latent].astype(F32),
                s_a[latent:].astype(F32), two, vec)

    return jax.shard_map(local_step, mesh=mesh, in_specs=in_specs, out_specs=out_specs, check_vma=False)
```

time: 480 us -> 199 us (0.41)
  Pallas kernels: 0 us -> 160 us
  waiting for transfers between devices: 133 us -> 0 us
  other arithmetic: 118 us -> 14.7 us
  matrix products: 97.6 us -> 0 us
  local copies, waits for them, and re-layouts: 79.3 us -> 23.2 us
  blocking collectives: 24 us -> 0 us
  between operations: 15.7 us -> 0.73 us
  starting transfers between devices: 7.75 us -> 0 us
    pallas_call x0 -> x2, Pallas kernels: none -> 160 us  [call(): pl.pallas_call(body, out_shape=outs, in_specs=[vm] * len(ins), out_specs=...]
    psum x1 -> x0, waiting for transfers between devices: 124 us -> none  [local_step(): weight_grads = lax.psum(weight_grads, AXIS_NAME)]
    dot_general x43 -> x0, matrix products: 97.6 us -> none  [the longest x15 36 us: matmul(): return jnp.dot(lhs, rhs, preferred_element_type=jnp.float32)]
    scatter-add x4 -> x0, other arithmetic: 65.7 us -> none  [the longest x1 18 us: local_step(): jax.ops.segment_sum(d_pre3_wide, edge_src, num_segments=slot_rows)]
    gather x5 -> x0, local copies, waits for them, and re-layouts: 35.9 us -> none  [the longest x2 13.2 us: local_step(): d_edge_new = jnp.take(d_agg, edge_dst, axis=0)]
    reduce_sum x17 -> x0, other arithmetic: 32.7 us -> none  [the longest x6 13.5 us: mlp_tail_back(): jnp.sum(d_lin, axis=0)]
    psum x1 -> x0, blocking collectives: 24 us -> none  [local_step(): weight_grads = lax.psum(weight_grads, AXIS_NAME)]
    unnamed x251 -> x27, local copies, waits for them, and re-layouts: 24 us -> 10.6 us
  transfers between devices with their start and end apart: 3 -> 0, of which waited for: 2 -> 0; matrix products, arithmetic and copies ran while one was open for 16% -> 0% of each run, Pallas kernels for 0% -> 0%
where the time goes in v1:
time: 199 us; the launch traced here: 198 us
  Pallas kernels  160 us (80%)
  local copies, waits for them, and re-layouts  23.2 us (12%)
  other arithmetic  14.7 us (7%)
    pallas_call x2, Pallas kernels, call(): pl.pallas_call(body, out_shape=outs, in_specs=[vm] * len(ins), out_specs=...  160 us
    unnamed x27, local copies, waits for them, and re-layouts  10.6 us

profile of v1, /device:TPU:0, one launch (start us, length us, event | category | flops | bytes accessed | tf_op | source)
XLA Modules:
  0.0 198.3 jit_solution(4907956000507761126)
XLA Ops:
  0.6 0.0 copy-start.6
  0.7 1.4 pad.9.mesh_static_t
  2.0 1.4 broadcast_in_dim_reshape.7.send_row
  3.4 1.3 broadcast_in_dim.6.src_row
  4.7 0.7 stack.30
  5.4 1.3 broadcast_in_dim.7.dst_row
  6.7 0.7 stack.31
  7.4 1.4 copy.45.mesh_static
  8.9 1.4 pad.8.edge_static_t
  10.2 1.8 copy.46.edge_static
  12.0 2.2 %broadcast_in_dim_reshape.8.send_col = s32[1536,1]{1,0:T(8,128)} reshape(s32[8,192]{1,0:T(8,128)} %param.19) | data formatting | bytes 12288 | tf_op jit(solution)/shard_map/broadcast_in_dim;reshape | solution.py:447
  14.2 1.4 copy.48.idx_col
  15.6 0.0 copy-done.6
  15.6 1.4 copy.44.grid_in
  17.0 34.3 %encode.1 = (bf16[1536,512]{1,0:T(8,128)(2,1)}, bf16[2304,512]{1,0:T(8,128)(2,1)}, bf16[128,512]{1,0:T(8,128)(2,1)}, bf16[1536,512]{1,0:T(8,128)(2,1)}, f32[1536...) custom-call(bf16[1536,272]{1,0:T(8,128)(2,1)} %copy.44.grid_in, bf16[128,3]{1,0:T(8,128)(2,1)} %copy.45.mesh_static, ...), custom_call_target="tpu_custom_call" | custom-call | tf_op jit(solution)/shard_map/encode/pallas_call | solution.py:440
  51.3 125.4 %update.1 = (bf16[128,512]{1,0:T(8,128)(2,1)}, f32[1536,272]{1,0:T(8,128)}, bf16[1024,512]{1,0:T(8,128)(2,1)}, bf16[1536,512]{1,0:T(8,128)(2,1)}, bf16[2048,512]...) custom-call(bf16[1536,512]{1,0:T(8,128)(2,1)} %get-tuple-element.25.incoming, ...), custom_call_target="tpu_custom_call" | custom-call | tf_op jit(solution)/shard_map/update/pallas_call | solution.py:440
  176.7 0.0 copy-start
  176.7 1.4 slice_convert_fusion.5
  178.2 1.3 slice_convert_fusion.6
  179.5 0.8 slice_bitcast_fusion
  180.3 0.6 slice_convert_fusion.4
  180.9 1.8 slice_convert_fusion.3
  182.7 0.0 copy-start.5
  182.7 2.2 %slice_convert_fusion.2 = f32[512,512]{1,0:T(8,128)} fusion(bf16[1024,512]{1,0:T(8,128)(2,1)} %get-tuple-element.37), kind=kLoop, calls=%fused_computation.8 | loop fusion | flops 262144 | bytes 1572864 | tf_op jit(solution)/shard_map/convert_element_type | solution.py:475
  185.0 0.0 copy-done
  185.0 1.7 copy.52
  186.7 0.0 copy-start.1
  186.7 0.0 copy-start.3
  186.7 0.0 copy-start.4
  186.7 1.2 bitcast_dynamic-update-slice_fusion.5
  187.9 0.0 copy-done.5
  188.0 0.4 copy-done.1
  188.5 0.4 copy-done.3
  188.9 0.3 copy-done.4
  189.2 1.6 slice_convert_fusion.1
  190.8 2.1 %slice_convert_fusion = f32[1536,512]{1,0:T(8,128)} fusion(bf16[2048,512]{1,0:T(8,128)(2,1)S(1)} %copy-done.1), kind=kLoop, calls=%fused_computation | loop fusion | flops 786432 | bytes 4718592 | tf_op jit(solution)/shard_map/convert_element_type | solution.py:474
  193.0 0.0 copy-start.7
  193.0 0.0 copy-start.2
  193.0 3.6 %convert_element_type.34 = f32[6,512,512]{2,1,0:T(8,128)} convert(bf16[6,512,512]{2,1,0:T(8,128)(2,1)S(1)} %bitcast_dynamic-update-slice_fusion) | non-fusion elementwise | flops 1572864 | bytes 9437184 | tf_op jit(solution)/shard_map/convert_element_type | solution.py:471
  196.5 0.0 copy-done.7
  196.5 0.7 copy.60
  197.2 0.0 copy-done.2
  197.2 1.1 copy.61
  (6 shorter events, 0.2 us)
Async XLA Ops:
  0.6 15.0 %copy-start.6 = (bf16[1536,272]{0,1:T(8,128)(2,1)S(1)}, bf16[1536,272]{0,1:T(8,128)(2,1)}, u32[]{:S(2)}) copy-start(bf16[1536,272]{0,1:T(8,128)(2,1)} %param.16) | copy-start | bytes 2506756
  176.7 8.3 %copy-start = (f32[1536,272]{1,0:T(8,128)S(1)}, f32[1536,272]{1,0:T(8,128)}, u32[]{:S(2)}) copy-start(f32[1536,272]{1,0:T(8,128)} %get-tuple-element.63) | copy-start | bytes 5013508
  182.7 5.2 %copy-start.5 = (bf16[1024,512]{1,0:T(8,128)(2,1)S(1)}, bf16[1024,512]{1,0:T(8,128)(2,1)}, u32[]{:S(2)}) copy-start(bf16[1024,512]{1,0:T(8,128)(2,1)} %get-tuple-element.38) | copy-start | bytes 3145732
  186.7 1.7 copy-start.1
  186.7 2.2 %copy-start.3 = (bf16[1536,512]{1,0:T(8,128)(2,1)S(1)}, bf16[1536,512]{1,0:T(8,128)(2,1)}, u32[]{:S(2)}) copy-start(bf16[1536,512]{1,0:T(8,128)(2,1)} %get-tuple-element.36) | copy-start | bytes 4718596
  186.7 2.5 %copy-start.4 = (bf16[1024,512]{1,0:T(8,128)(2,1)S(1)}, bf16[1024,512]{1,0:T(8,128)(2,1)}, u32[]{:S(2)}) copy-start(bf16[1024,512]{1,0:T(8,128)(2,1)} %get-tuple-element.37) | copy-start | bytes 3145732
  193.0 3.6 %copy-start.7 = (bf16[128,512]{1,0:T(8,128)(2,1)S(1)}, bf16[128,512]{1,0:T(8,128)(2,1)}, u32[]{:S(2)}) copy-start(bf16[128,512]{1,0:T(8,128)(2,1)} %get-tuple-element.83) | copy-start | bytes 393220
  193.0 4.2 %copy-start.2 = (bf16[1536,512]{1,0:T(8,128)(2,1)S(1)}, bf16[1536,512]{1,0:T(8,128)(2,1)}, u32[]{:S(2)}) copy-start(bf16[1536,512]{1,0:T(8,128)(2,1)} %get-tuple-element.84) | copy-start | bytes 4718596
